TPU v7x, 32 devices: a whole 2x2x4 slice. The times are simulated.
32 devices in a mesh: ba: 8 (over y, x, core), wa: 4 (over z).
Axes of the slice: x: 2, y: 2, z: 4, core: 2. Of those that a mesh axis runs over, the one named last changes fastest.
Arguments:
- sky_model: float32 [2, 2048, 2048], P(None, None, 'wa'), may hold values from -6 to 6
- plane_w: float32 [8], P('ba'), may hold values from -60 to 60
- kernel: float32 [16, 8], replicated, may hold values from -2 to 2
- tile_ids: int32 [512], P(('ba', 'wa')), may hold values from 0 to 255, as said below
- plane_ids: int32 [512, 1], P(('ba', 'wa')), may hold values from 0 to 7; in each aligned block of 16 rows (0 to 15, 16 to 31, ...) at most 2 rows name the same one
- positions: int32 [512, 2, 512], P(('ba', 'wa')), may hold values from 0 to 1935
- observed: float32 [512, 2, 512], P(('ba', 'wa')), may hold values from -6 to 6
Outputs:
- residual_vis: float32 [512, 2, 512], P(('ba', 'wa'))
Inputs may be any that keep to these rules, and one draw needn't show every extreme that they name: `plane_ids`: among the 16 blocks of one device at most 2 name the same w-plane, and in every draw some device has a w-plane named by exactly 2 of its blocks. `tile_ids`: A tile id is row_tile * 16 + column_tile; the blocks held at index a of wa name column tiles a * 4 to (a + 1) * 4 - 1.
All inputs are finite; a program needn't handle non-finite values.
Results may differ from a plain program's by a relative error of at most 0.0003.
Values sent between devices are 32-bit elements; how exact they have to be, the bound alone decides.
A program may use at most 128 MiB of HBM per device.

v0:
```python
import math

import jax
import jax.numpy as jnp
from jax import lax
from jax.sharding import PartitionSpec as P

TILE = 128


PRECISE = lax.Precision.HIGHEST
FIELD_WIDTH = 0.7


def product(pattern, operand_a, operand_b):
    return jnp.einsum(pattern, operand_a, operand_b, precision=PRECISE)


def complex_product(pattern, table_pair, values):
    return (
        product(pattern, table_pair[0], values[0]) - product(pattern, table_pair[1], values[1]),
        product(pattern, table_pair[0], values[1]) + product(pattern, table_pair[1], values[0]),
    )


def phase_table(rows_count, cols_count, modulus):
    first_index = jnp.arange(rows_count, dtype=jnp.int32)[:, None]
    second_index = jnp.arange(cols_count, dtype=jnp.int32)[None, :]
    angle_rad = (first_index * second_index % modulus).astype(jnp.float32) * (
        -2.0 * math.pi / modulus
    )
    return (jnp.cos(angle_rad), jnp.sin(angle_rad))


def transform(values, pattern):
    length = values[0].shape[0]
    columns = values[0].shape[1]
    long_side = min(length, 128)
    short_side = length // long_side
    shaped = (
        values[0].reshape(long_side, short_side, columns),
        values[1].reshape(long_side, short_side, columns),
    )
    section_one = complex_product(
        "ab,anl->bnl", phase_table(long_side, long_side, long_side), shaped
    )
    twiddle = phase_table(long_side, short_side, length)
    twist_real = twiddle[0][:, :, None]
    twist_imag = twiddle[1][:, :, None]
    turned = (
        section_one[0] * twist_real - section_one[1] * twist_imag,
        section_one[0] * twist_imag + section_one[1] * twist_real,
    )
    return complex_product(
        "nk,bnl->" + pattern, phase_table(short_side, short_side, short_side), turned
    )


def kernel_rows(fine_position, kernel, tile_side):
    oversample, support = kernel.shape
    cell_index = fine_position // oversample
    offset_index = fine_position % oversample
    picker = (offset_index[..., None] == jnp.arange(oversample, dtype=jnp.int32)).astype(
        jnp.float32
    )
    kernel_taps = product("gso,ok->gsk", picker, kernel)
    tile_cells = jnp.arange(tile_side, dtype=jnp.int32)
    weights = jnp.zeros(fine_position.shape + (tile_side,), jnp.float32)
    for tap_step in range(support):
        weights = weights + jnp.where(
            tile_cells == cell_index[..., None] + tap_step,
            kernel_taps[..., tap_step : tap_step + 1],
            0.0,
        )
    return weights


def degrid(tiles, fine_position, kernel):
    tile_side = tiles.shape[-1]
    row_weights = kernel_rows(fine_position[:, 0], kernel, tile_side)
    col_weights = kernel_rows(fine_position[:, 1], kernel, tile_side)
    partial_value = product("gsu,gcuv->gcsv", row_weights, tiles)
    return jnp.sum(partial_value * col_weights[:, None], axis=-1)


def grouped(function, count, operands):
    group_size = math.gcd(count, 8)
    reshaped = tuple(
        (
            operand.reshape((count // group_size, group_size) + operand.shape[1:])
            for operand in operands
        )
    )

    def apply_group(group_items):
        return function(*group_items)

    result = lax.map(apply_group, reshaped)
    return result.reshape((count,) + result.shape[2:])


def shards(sky_model, plane_w, kernel, tile_ids, plane_ids, positions, observed):
    extent = sky_model.shape[1]
    column_count = sky_model.shape[2]
    slab_index = lax.axis_index("wa")
    spacing = FIELD_WIDTH / extent
    column_coord = (
        (slab_index * column_count + jnp.arange(column_count, dtype=jnp.int32)).astype(jnp.float32)
        - extent / 2
    ) * spacing
    row_coord = (jnp.arange(extent, dtype=jnp.int32).astype(jnp.float32) - extent / 2) * spacing
    radius_sq = row_coord[:, None] ** 2 + column_coord[None, :] ** 2
    lowered = -radius_sq / (1.0 + jnp.sqrt(1.0 - radius_sq))
    phase_angle = -2.0 * math.pi * plane_w[0] * lowered
    cosine = jnp.cos(phase_angle)
    sine_part = jnp.sin(phase_angle)
    image_real = sky_model[0] * cosine - sky_model[1] * sine_part
    image_imag = sky_model[0] * sine_part + sky_model[1] * cosine
    half_done = transform((image_real, image_imag), "lkb")
    stacked = jnp.stack(
        [half_done[0].reshape(column_count, extent), half_done[1].reshape(column_count, extent)]
    )
    exchanged = lax.all_to_all(stacked, "wa", split_axis=2, concat_axis=1, tiled=True)
    finished = transform((exchanged[0], exchanged[1]), "kbl")
    norm_factor = 1.0 / extent
    uv_grid = jnp.stack(
        [
            finished[0].reshape(extent, column_count) * norm_factor,
            finished[1].reshape(extent, column_count) * norm_factor,
        ]
    )
    plane_count = lax.axis_size("ba")
    block_count = tile_ids.shape[0]
    sample_count = positions.shape[2]
    capacity = max(2, block_count // plane_count)
    target = plane_ids[:, 0]
    onehot = (target[:, None] == jnp.arange(plane_count, dtype=jnp.int32)[None, :]).astype(
        jnp.int32
    )
    earlier = jnp.cumsum(onehot, axis=0) - onehot
    rank_in = jnp.sum(earlier * onehot, axis=1)
    slot_index = target * capacity + rank_in
    slot_tiles = jnp.zeros((plane_count * capacity,), jnp.int32).at[slot_index].set(tile_ids)
    slot_tiles = slot_tiles.reshape(plane_count, capacity)
    tile_side = TILE
    tiles_across = extent // tile_side
    local_across = column_count // tile_side

    def cut_tile(tile_number):
        row_tile = tile_number // tiles_across
        col_tile = tile_number % tiles_across - slab_index * local_across
        return lax.dynamic_slice(
            uv_grid,
            (jnp.int32(0), row_tile * tile_side, col_tile * tile_side),
            (2, tile_side, tile_side),
        )

    slot_fine = (
        jnp.zeros((plane_count * capacity, 2, sample_count), jnp.int32)
        .at[slot_index]
        .set(positions)
    )
    slot_fine = slot_fine.reshape(plane_count, capacity, 2, sample_count)
    asked_tiles = lax.all_to_all(slot_tiles, "ba", split_axis=0, concat_axis=0, tiled=True)
    asked_fine = lax.all_to_all(slot_fine, "ba", split_axis=0, concat_axis=0, tiled=True)
    count = asked_tiles.shape[0] * asked_tiles.shape[1]

    def slot_group(tile_group, fine_group):
        return degrid(jax.vmap(cut_tile)(tile_group), fine_group, kernel)

    values = grouped(
        slot_group, count, (asked_tiles.reshape(count), asked_fine.reshape(count, 2, sample_count))
    )
    values = values.reshape(asked_tiles.shape[0], asked_tiles.shape[1], 2, sample_count)
    answers = lax.all_to_all(values, "ba", split_axis=0, concat_axis=0, tiled=True)
    predicted = answers.reshape(plane_count * capacity, 2, sample_count)[slot_index]
    return observed - predicted


def solution(mesh):
    return jax.shard_map(
        shards,
        mesh=mesh,
        in_specs=(
            P(None, None, "wa"),
            P("ba"),
            P(),
            P(("ba", "wa")),
            P(("ba", "wa"), None),
            P(("ba", "wa"), None, None),
            P(("ba", "wa"), None, None),
        ),
        out_specs=P(("ba", "wa"), None, None),
        check_vma=False,
    )
```

profile of v0, /device:TPU:0, one launch (start us, length us, event | category | flops | bytes accessed | tf_op | source)
XLA Modules:
  0.0 575.9 jit_solution(2095315293875353910)
XLA Ops:
  3.7 5.2 all-to-all-start
  9.0 7.7 %fusion.226 = (f32[1,2048,512]{2,1,0:T(8,128)}, f32[1,2048,512]{2,1,0:T(8,128)}) fusion(f32[2,2048,512]{2,1,0:T(8,128)} %param.9), kind=kLoop, calls=%fused_computation.309 | loop fusion | bytes 16777216 | tf_op jit(solution)/shard_map/slice | solution.py:117
  17.3 34.6 %fusion.105 = f32[128,16,512]{2,0,1:T(8,128)S(1)} fusion(f32[128,16,512]{2,1,0:T(8,128)} %bitcast.269, f32[128,16,512]{2,1,0:T(8,128)} %bitcast.265, f32[512]{0:T(512)S(1)} %multiply_multiply_fusion.1, f32[128,16]{0,1:T(8,128)S(1)} %get-tuple-element.237, f32[]{:T(128)} %bitcast.16), kind=kOutput, calls=%fused_computation.193 | convolution fusion | flops 1620279296 | bytes 12593156 | tf_op jit(solution)/shard_map/ab,anl->bnl/dot_general | solution.py:16
  51.9 23.6 %fusion.103 = f32[128,16,512]{2,0,1:T(8,128)S(1)} fusion(f32[128,16,512]{2,1,0:T(8,128)S(1)} %bitcast.270, f32[128,16,512]{2,1,0:T(8,128)S(1)} %bitcast.266, f32[512]{0:T(512)S(1)} %multiply_multiply_fusion.1, f32[128,16]{0,1:T(8,128)S(1)} %get-tuple-element.237, f32[]{:T(128)} %bitcast.16), kind=kOutput, calls=%fused_computation.191 | convolution fusion | flops 1620279296 | bytes 12593156 | tf_op jit(solution)/shard_map/ab,anl->bnl/dot_general | solution.py:16
  75.6 24.7 %convolution_subtract_fusion = f32[128,16,512]{2,0,1:T(8,128)} fusion(f32[128,16,512]{2,0,1:T(8,128)S(1)} %fusion.105, f32[128,16,512]{2,1,0:T(8,128)S(1)} %bitcast.271, f32[128,16,512]{2,1,0:T(8,128)S(1)} %bitcast.267, f32[512]{0:T(512)S(1)} %multiply_multiply_fusion.1, f32[128,16]{0,1:T(8,128)S(1)} %get-tuple-element.237, f32[]{:T(128)} %bitcast.16), kind=kOutput, calls=%fused_computation.176 | convolution fusion | flops 1621327872 | bytes 16787460 | tf_op jit(solution)/shard_map/ab,anl->bnl/dot_general | solution.py:16
  100.3 25.9 %multiply_subtract_fusion.1 = (f32[128,16,512]{2,0,1:T(8,128)S(1)}, f32[128,16,512]{2,0,1:T(8,128)S(1)}) fusion(f32[128,16,512]{2,0,1:T(8,128)} %convolution_subtract_fusion, f32[128,16]{0,1:T(8,128)S(1)} %get-tuple-element.238, f32[128,16]{0,1:T(8,128)S(1)} %fusion.142, f32[128,16,512]{2,0,1:T(8,128)S(1)} %fusion.103, f32[128,16,512]{2,1,0:T(8,128)S(1)} %bitcast.272, ...), kind=kOutput, calls=%fused_computation.146 | convolution fusion | flops 1627619328 | bytes 25192452 | tf_op jit(solution)/shard_map/ab,anl->bnl/dot_general | solution.py:16
  126.3 6.6 %fusion.72 = f32[128,512,16]{1,2,0:T(8,128)S(1)} fusion(f32[128,16,512]{2,0,1:T(8,128)S(1)} %get-tuple-element.232), kind=kOutput, calls=%fused_computation.167 | convolution fusion | flops 201330176 | bytes 8388608 | tf_op jit(solution)/shard_map/nk,bnl->lkb/dot_general | solution.py:16
  132.8 6.8 %fusion.70 = f32[128,512,16]{1,2,0:T(8,128)S(1)} fusion(f32[128,16,512]{2,0,1:T(8,128)S(1)} %get-tuple-element.232), kind=kOutput, calls=%fused_computation.165 | convolution fusion | flops 201330176 | bytes 8388608 | tf_op jit(solution)/shard_map/nk,bnl->lkb/dot_general | solution.py:16
  139.7 7.1 %subtract_bitcast_fusion = f32[512,16,128]{0,1,2:T(8,128)S(1)} fusion(f32[128,512,16]{1,2,0:T(8,128)S(1)} %fusion.72, f32[128,16,512]{2,0,1:T(8,128)S(1)} %get-tuple-element.231), kind=kOutput, calls=%fused_computation.144 | convolution fusion | flops 202378752 | bytes 12582912 | tf_op jit(solution)/shard_map/nk,bnl->lkb/dot_general | solution.py:16
  149.2 7.4 %add_bitcast_fusion = f32[512,16,128]{0,1,2:T(8,128)S(1)} fusion(f32[128,512,16]{1,2,0:T(8,128)S(1)} %fusion.70, f32[128,16,512]{2,0,1:T(8,128)S(1)} %get-tuple-element.231), kind=kOutput, calls=%fused_computation.143 | convolution fusion | flops 202378752 | bytes 12582912 | tf_op jit(solution)/shard_map/nk,bnl->lkb/dot_general | solution.py:16
  160.0 16.5 %copy.84 = f32[2,512,2048]{1,0,2:T(2,128)} copy(f32[2,512,2048]{1,2,0:T(8,128)S(1)} %pad_maximum_fusion) | data formatting | bytes 16777216 | tf_op jit(solution)/shard_map/stack | solution.py:120
  176.5 5.8 %all-to-all-start.1 = ((f32[2,512,2048]{1,0,2:T(2,128)}), f32[2,512,2048]{1,0,2:T(2,128)}, u32[]{:S(2)}, u32[]{:S(2)}) async-start(f32[2,512,2048]{1,0,2:T(2,128)} %copy.84), calls=%async_computation.1 | async-start | bytes 16777216 | tf_op jit(solution)/shard_map/all_to_all | solution.py:123
  186.4 180.0 %all-to-all-done.1 = f32[2,512,2048]{1,0,2:T(2,128)} async-done(((f32[2,512,2048]{1,0,2:T(2,128)}), f32[2,512,2048]{1,0,2:T(2,128)}, u32[]{:S(2)}, u32[]{:S(2)}) %all-to-all-start.1) | async-done | bytes 8388640 | tf_op jit(solution)/shard_map/all_to_all | solution.py:123
  370.3 5.0 copy.85
  379.6 5.3 copy.88
  384.9 10.2 %fusion.64 = f32[128,16,512]{2,0,1:T(8,128)} fusion(f32[128,16,512]{2,1,0:T(8,128)} %bitcast.256), kind=kOutput, calls=%fused_computation.159 | convolution fusion | flops 1610842112 | bytes 8388608 | tf_op jit(solution)/shard_map/ab,anl->bnl/dot_general | solution.py:16
  395.1 7.1 %fusion.62 = f32[128,16,512]{2,0,1:T(8,128)} fusion(f32[128,16,512]{2,1,0:T(8,128)S(1)} %bitcast.257), kind=kOutput, calls=%fused_computation.157 | convolution fusion | flops 1610842112 | bytes 8388608 | tf_op jit(solution)/shard_map/ab,anl->bnl/dot_general | solution.py:16
  402.3 5.6 copy.86
  407.9 9.9 %fusion.82 = f32[128,16,512]{2,0,1:T(8,128)S(1)} fusion(f32[128,16,512]{2,0,1:T(8,128)} %fusion.64, f32[128,16,512]{2,1,0:T(8,128)} %bitcast.254), kind=kOutput, calls=%fused_computation.173 | convolution fusion | flops 1611890688 | bytes 12582912 | tf_op jit(solution)/shard_map/ab,anl->bnl/dot_general | solution.py:16
  417.8 7.5 %multiply_subtract_fusion = (f32[128,16,512]{2,0,1:T(8,128)S(1)}, f32[128,16,512]{2,0,1:T(8,128)S(1)}) fusion(f32[128,16,512]{2,0,1:T(8,128)S(1)} %fusion.82, f32[128,16]{0,1:T(8,128)S(1)} %get-tuple-element.238, f32[128,16]{0,1:T(8,128)S(1)} %fusion.142, f32[128,16,512]{2,0,1:T(8,128)S(1)} %copy-done.2, f32[128,16,512]{2,1,0:T(8,128)S(1)} %bitcast.255), kind=kOutput, calls=%fused_computation.142 | convolution fusion | flops 1618182144 | bytes 20987904 | tf_op jit(solution)/shard_map/ab,anl->bnl/dot_general | solution.py:16
  425.3 5.6 fusion.56
  430.9 5.8 %fusion.54 = f32[16,128,512]{2,0,1:T(8,128)S(1)} fusion(f32[128,16,512]{2,0,1:T(8,128)S(1)} %get-tuple-element.230), kind=kOutput, calls=%fused_computation.149 | convolution fusion | flops 201330176 | bytes 8388608 | tf_op jit(solution)/shard_map/nk,bnl->kbl/dot_general | solution.py:16
  436.7 6.1 %subtract_multiply_fusion = f32[16,128,512]{2,0,1:T(8,128)S(1)} fusion(f32[16,128,512]{2,0,1:T(8,128)S(1)} %fusion.56, f32[128,16,512]{2,0,1:T(8,128)S(1)} %get-tuple-element.229), kind=kOutput, calls=%fused_computation.140 | convolution fusion | flops 203427328 | bytes 12582912 | tf_op jit(solution)/shard_map/nk,bnl->kbl/dot_general | solution.py:16
  445.2 6.0 %add_multiply_fusion = f32[16,128,512]{2,0,1:T(8,128)S(1)} fusion(f32[16,128,512]{2,0,1:T(8,128)S(1)} %fusion.54, f32[128,16,512]{2,0,1:T(8,128)S(1)} %get-tuple-element.229), kind=kOutput, calls=%fused_computation.139 | convolution fusion | flops 203427328 | bytes 12582912 | tf_op jit(solution)/shard_map/nk,bnl->kbl/dot_general | solution.py:16
  457.9 107.2 %while.16 = (s32[]{:T(128)}, f32[2,8,2,512]{3,2,1,0:T(2,128)}, s32[2,8]{1,0:T(2,128)S(1)}, s32[]{:T(128)}, f32[2,2048,512]{2,1,0:T(8,128)}, /*index=5*/s32[2,8,2...) while((s32[]{:T(128)}, f32[2,8,2,512]{3,2,1,0:T(2,128)}, ...), condition=%wide.region_6.7_spmd, body=%wide.region_4.6_spmd.sunk | while | flops 1649795328 | bytes 12208282 | solution.py:98
  458.4 8.9 %select_add_fusion.2 = f32[8,512,128]{2,1,0:T(8,128)S(1)} fusion(f32[8,512]{1,0:T(8,128)S(1)} %bitcast.273, s32[8,512]{1,0:T(8,128)S(1)} %get-tuple-element.360, f32[8,512]{1,0:T(8,128)S(1)} %bitcast.274, s32[8,512]{1,0:T(8,128)S(1)} %get-tuple-element.362, f32[8,512]{1,0:T(8,128)S(1)} %bitcast.275, s32[8,512]{1,0:T(8,128)S(1)} %get-tuple-element.364, ...), kind=kLoop, calls=%fused_computation.8.clone.1 | loop fusion | flops 12058624 | bytes 2359296 | tf_op jit(solution)/shard_map/while/body/eval_jaxpr/add | solution.py:70
  469.7 23.6 %while.17 = (s32[]{:T(128)}, f32[2,2048,512]{2,1,0:T(8,128)}, s32[8,3]{0,1:T(4,128)S(1)}, f32[8,2,128,128]{3,2,1,0:T(8,128)S(1)}, s32[]{:T(128)}) while((s32[]{:T(128)}, f32[2,2048,512]{2,1,0:T(8,128)}, s32[8,3]{0,1:T(4,128)S(1)}, f32[8,2,128,128]{3,2,1,0:T(8,128)S(1)}, s32[]{:T(128)}) %tuple.108), condition=%wide.while_cond, body=%wide.while_body.sunk | while | flops 2 | bytes 262261 | solution.py:152
  493.3 17.5 %fusion.249 = f32[8,2,512]{2,1,0:T(2,128)S(1)} fusion(f32[8,2,128,128]{3,2,1,0:T(8,128)S(1)} %get-tuple-element.354, f32[8,512,128]{1,2,0:T(8,128)} %copy.239, f32[8,512]{1,0:T(8,128)S(1)} %bitcast.282, s32[8,512]{1,0:T(8,128)S(1)} %get-tuple-element.377, f32[8,512]{1,0:T(8,128)S(1)} %bitcast.283, s32[8,512]{1,0:T(8,128)S(1)} %get-tuple-element.379, ...), kind=kOutput, calls=%fused_computation.6.clone.2 | convolution fusion | flops 1624760320 | bytes 3440640 | tf_op jit(solution)/shard_map/while/body/eval_jaxpr/gsu,gcuv->gcsv/dot_general | solution.py:16
  511.9 8.9 %select_add_fusion.2 = f32[8,512,128]{2,1,0:T(8,128)S(1)} fusion(f32[8,512]{1,0:T(8,128)S(1)} %bitcast.273, s32[8,512]{1,0:T(8,128)S(1)} %get-tuple-element.360, f32[8,512]{1,0:T(8,128)S(1)} %bitcast.274, s32[8,512]{1,0:T(8,128)S(1)} %get-tuple-element.362, f32[8,512]{1,0:T(8,128)S(1)} %bitcast.275, s32[8,512]{1,0:T(8,128)S(1)} %get-tuple-element.364, ...), kind=kLoop, calls=%fused_computation.8.clone.1 | loop fusion | flops 12058624 | bytes 2359296 | tf_op jit(solution)/shard_map/while/body/eval_jaxpr/add | solution.py:70
  523.3 23.8 %while.17 = (s32[]{:T(128)}, f32[2,2048,512]{2,1,0:T(8,128)}, s32[8,3]{0,1:T(4,128)S(1)}, f32[8,2,128,128]{3,2,1,0:T(8,128)S(1)}, s32[]{:T(128)}) while((s32[]{:T(128)}, f32[2,2048,512]{2,1,0:T(8,128)}, s32[8,3]{0,1:T(4,128)S(1)}, f32[8,2,128,128]{3,2,1,0:T(8,128)S(1)}, s32[]{:T(128)}) %tuple.108), condition=%wide.while_cond, body=%wide.while_body.sunk | while | flops 2 | bytes 262261 | solution.py:152
  547.0 17.5 %fusion.249 = f32[8,2,512]{2,1,0:T(2,128)S(1)} fusion(f32[8,2,128,128]{3,2,1,0:T(8,128)S(1)} %get-tuple-element.354, f32[8,512,128]{1,2,0:T(8,128)} %copy.239, f32[8,512]{1,0:T(8,128)S(1)} %bitcast.282, s32[8,512]{1,0:T(8,128)S(1)} %get-tuple-element.377, f32[8,512]{1,0:T(8,128)S(1)} %bitcast.283, s32[8,512]{1,0:T(8,128)S(1)} %get-tuple-element.379, ...), kind=kOutput, calls=%fused_computation.6.clone.2 | convolution fusion | flops 1624760320 | bytes 3440640 | tf_op jit(solution)/shard_map/while/body/eval_jaxpr/gsu,gcuv->gcsv/dot_general | solution.py:16
  569.2 5.0 all-to-all-done.3
  (157 shorter events, 90.0 us)
Async XLA Ops:
  3.7 172.8 %all-to-all-start = ((s32[8,1,2]{2,1,0:T(1,128)}), s32[8,1,2]{2,1,0:T(1,128)S(1)}, u32[]{:S(2)}, u32[]{:S(2)}) async-start(s32[8,1,2]{2,1,0:T(1,128)} %bitcast.12), calls=%async_computation | async-start | bytes 8192 | tf_op jit(solution)/shard_map/all_to_all | solution.py:164
  17.3 34.6 %copy-start.3 = (f32[1,2048,512]{2,1,0:T(8,128)S(1)}, f32[1,2048,512]{2,1,0:T(8,128)}, u32[]{:S(2)}) copy-start(f32[1,2048,512]{2,1,0:T(8,128)} %get-tuple-element.235) | copy-start | bytes 12582916
  17.3 34.6 %copy-start.4 = (f32[1,2048,512]{2,1,0:T(8,128)S(1)}, f32[1,2048,512]{2,1,0:T(8,128)}, u32[]{:S(2)}) copy-start(f32[1,2048,512]{2,1,0:T(8,128)} %get-tuple-element.236) | copy-start | bytes 12582916
  176.5 6.4 %copy-start.6 = (s32[16,2,512]{2,1,0:T(2,128)S(1)}, s32[16,2,512]{2,1,0:T(2,128)}, u32[]{:S(2)}) copy-start(s32[16,2,512]{2,1,0:T(2,128)} %param.14) | copy-start | bytes 196612
  176.5 189.8 %all-to-all-start.1 = ((f32[2,512,2048]{1,0,2:T(2,128)}), f32[2,512,2048]{1,0,2:T(2,128)}, u32[]{:S(2)}, u32[]{:S(2)}) async-start(f32[2,512,2048]{1,0,2:T(2,128)} %copy.84), calls=%async_computation.1 | async-start | bytes 16777216 | tf_op jit(solution)/shard_map/all_to_all | solution.py:123
  366.3 91.6 %all-to-all-start.2 = ((s32[8,2,2,512]{3,2,1,0:T(2,128)}), s32[8,2,2,512]{3,2,1,0:T(2,128)S(1)}, u32[]{:S(2)}, u32[]{:S(2)}) async-start(s32[8,2,2,512]{3,2,1,0:T(2,128)} %bitcast.31), calls=%async_computation.2 | async-start | bytes 131072 | tf_op jit(solution)/shard_map/all_to_all | solution.py:165
  384.9 10.2 %copy-start.1 = (f32[1,4,512,512]{3,2,1,0:T(8,128)S(1)}, f32[1,4,512,512]{3,2,1,0:T(8,128)}, u32[]{:S(2)}) copy-start(f32[1,4,512,512]{3,2,1,0:T(8,128)} %copy.88) | copy-start | bytes 12582916
  407.9 9.9 %copy-start = (f32[1,4,512,512]{3,2,1,0:T(8,128)S(1)}, f32[1,4,512,512]{3,2,1,0:T(8,128)}, u32[]{:S(2)}) copy-start(f32[1,4,512,512]{3,2,1,0:T(8,128)} %copy.86) | copy-start | bytes 12582916
  407.9 9.9 %copy-start.2 = (f32[128,16,512]{2,0,1:T(8,128)S(1)}, f32[128,16,512]{2,0,1:T(8,128)}, u32[]{:S(2)}) copy-start(f32[128,16,512]{2,0,1:T(8,128)} %fusion.62) | copy-start | bytes 12582916
  453.7 4.2 copy-start.5
  457.9 116.9 %copy-start.7 = (f32[16,2,512]{2,1,0:T(2,128)S(1)}, f32[16,2,512]{2,1,0:T(2,128)}, u32[]{:S(2)}) copy-start(f32[16,2,512]{2,1,0:T(2,128)} %param.15) | copy-start | bytes 196612
  565.1 9.1 %all-to-all-start.3 = ((f32[8,2,2,512]{3,2,1,0:T(2,128)}), f32[8,2,2,512]{3,2,1,0:T(2,128)S(1)}, u32[]{:S(2)}, u32[]{:S(2)}) async-start(f32[8,2,2,512]{3,2,1,0:T(2,128)} %bitcast.33), calls=%async_computation.3 | async-start | bytes 131072 | tf_op jit(solution)/shard_map/all_to_all | solution.py:175
where the time goes:
time: 583 us; the launch traced here: 576 us
  matrix products  231 us (40%)
  waiting for transfers between devices  185 us (32%)
  local copies, waits for them, and re-layouts  112 us (19%)
  other arithmetic  27.1 us (5%)
  starting transfers between devices  19 us (3%)
    dot_general x22, matrix products, product(): return jnp.einsum(pattern, operand_a, operand_b, precision=PRECISE)  231 us
    all_to_all x1, waiting for transfers between devices, shards(): lax.all_to_all(stacked, 'wa', split_axis=2, concat_axis=1, tiled=True)  180 us
    gather x48, local copies, waits for them, and re-layouts  47.1 us
    add x2, other arithmetic, kernel_rows(): weights + jnp.where(tile_cells == cell_index[..., None] + tap_step, kerne...  17.9 us
    another operation x1, local copies, waits for them, and re-layouts, shards(): jnp.stack([half_done[0].reshape(column_count, extent), half_done[1].resha...  16.5 us
    slice x3, local copies, waits for them, and re-layouts, shards(): finished = transform((exchanged[0], exchanged[1]), 'kbl')  15.2 us
  transfers between devices with their start and end apart: 4, of which 2 were waited for; matrix products, arithmetic and copies ran while one was open for 45% of the time, Pallas kernels for 0%

commit v1 on v0

v1 whole, which is shorter than its diff:
```python
import functools
import math

import jax
import jax.numpy as jnp
import numpy as np
from jax import lax
from jax.experimental import pallas as pl
from jax.experimental.pallas import tpu as pltpu
from jax.sharding import PartitionSpec as P

TILE = 128
FIELD_WIDTH = 0.7


def halves(values):
    head = values.astype(jnp.bfloat16)
    rest = (values - head.astype(jnp.float32)).astype(jnp.bfloat16)
    return head, rest


def host_halves(values):
    values = values.astype(np.float32)
    head = values.astype(jnp.bfloat16)
    rest = (values - head.astype(np.float32)).astype(jnp.bfloat16)
    return head, rest


def roots(index, modulus):
    angle = -2.0 * np.pi * (index % modulus) / modulus
    return np.cos(angle), np.sin(angle)


def y_tables(extent):
    panels = extent // TILE
    residue = np.arange(panels, dtype=np.int64)[:, None, None]
    step = np.arange(TILE, dtype=np.int64)[None, :, None]
    row = np.arange(TILE, dtype=np.int64)[None, None, :]
    real, imag = roots((panels * step + residue) * row, extent)
    table = np.concatenate(
        [np.concatenate([real, -imag], axis=2), np.concatenate([imag, real], axis=2)], axis=1
    )
    return host_halves(table)


def x_tables(extent, columns):
    tiles = np.arange(extent // TILE, dtype=np.int64)[:, None, None]
    column = np.arange(columns, dtype=np.int64)[None, :, None]
    cell = np.arange(TILE, dtype=np.int64)[None, None, :]
    real, imag = roots((tiles * TILE + cell) * column, extent)
    return host_halves(np.concatenate([real, imag], axis=2))


def fit(function, top, terms):
    nodes = (np.cos((np.arange(400) + 0.5) * np.pi / 400) + 1.0) * 0.5 * top
    series = np.polynomial.chebyshev.Chebyshev.fit(nodes, function(nodes), terms - 1, domain=[0, top])
    return [float(c) for c in series.convert(kind=np.polynomial.Polynomial).coef]


def horner(coefficients, argument):
    total = coefficients[-1]
    for coefficient in coefficients[-2::-1]:
        total = total * argument + coefficient
    return total


def small_dft(values):
    count = len(values)
    if count == 1:
        return values
    even = small_dft(values[0::2])
    odd = small_dft(values[1::2])
    low, high = [], []
    for k in range(count // 2):
        real, imag = odd[k]
        if k == 0:
            pass
        elif 4 * k == count:
            real, imag = imag, -real
        elif 8 * k == count:
            h = math.sqrt(0.5)
            real, imag = (real + imag) * h, (imag - real) * h
        elif 8 * k == 3 * count:
            h = math.sqrt(0.5)
            real, imag = (imag - real) * h, (real + imag) * -h
        else:
            c = math.cos(-2.0 * math.pi * k / count)
            s = math.sin(-2.0 * math.pi * k / count)
            real, imag = real * c - imag * s, real * s + imag * c
        low.append((even[k][0] + real, even[k][1] + imag))
        high.append((even[k][0] - real, even[k][1] - imag))
    return low + high


def y_kernel(extent, columns, w_ref, sky_ref, head_ref, rest_ref, out_head, out_rest, work):
    panels = extent // TILE
    lanes = sky_ref.shape[2]
    spacing = FIELD_WIDTH / extent
    first = lax.axis_index("wa") * columns + pl.program_id(0) * lanes
    w = w_ref[0]
    edge = 2.0 * (FIELD_WIDTH / 2) ** 2
    lower = fit(lambda r: 1.0 / (1.0 + np.sqrt(1.0 - r)), edge, 7)
    sine = fit(lambda z: np.sin(2 * np.pi * np.sqrt(z)) / np.sqrt(z), 0.25, 7)
    cosine = fit(lambda z: np.cos(2 * np.pi * np.sqrt(z)), 0.25, 7)

    for lane in range(0, lanes, 128):
        x = lax.broadcasted_iota(jnp.int32, (8, 128), 1) + (first + lane)
        x = (x.astype(jnp.float32) - extent / 2) * spacing
        x_sq = x * x

        @pl.loop(0, TILE // 8)
        def _(group):
            base = pl.multiple_of(group * 8, 8)
            values = []
            for panel in range(panels):
                row = lax.broadcasted_iota(jnp.int32, (8, 128), 0) + (base + panel * TILE)
                y = (row.astype(jnp.float32) - extent / 2) * spacing
                radius = x_sq + y * y
                turns = radius * horner(lower, radius) * w
                turns = turns - jnp.round(turns)
                square = turns * turns
                s = turns * horner(sine, square)
                c = horner(cosine, square)
                real = sky_ref[0, pl.ds(base + panel * TILE, 8), pl.ds(lane, 128)]
                imag = sky_ref[1, pl.ds(base + panel * TILE, 8), pl.ds(lane, 128)]
                values.append((real * c - imag * s, real * s + imag * c))
            for residue, (real, imag) in enumerate(small_dft(values)):
                work[residue, pl.ds(base, 8), pl.ds(lane, 128)] = real
                work[residue, pl.ds(base + TILE, 8), pl.ds(lane, 128)] = imag

    def panel_product(residue):
        head, rest = halves(work[residue])
        dot = functools.partial(jnp.dot, preferred_element_type=jnp.float32)
        table = head_ref[residue]
        return dot(table, head) + dot(table, rest) + dot(rest_ref[residue], head)

    per_tile = TILE // panels
    share = 8 // per_tile
    together = 16 // per_tile

    @pl.loop(0, panels // together)
    def _(step):
        products = [panel_product(together * step + i) for i in range(together)]
        for part in range(2):
            rows = slice(part * TILE, (part + 1) * TILE)
            grouped = [product[rows].reshape(TILE // 8, 8, lanes) for product in products]
            at = pl.multiple_of(part * TILE + step * 16, 16)
            for place in range(share):
                cut = slice(place * per_tile, (place + 1) * per_tile)
                head, rest = halves(jnp.concatenate([group[:, cut] for group in grouped], axis=1))
                out_head[:, place, pl.ds(at, 16), :] = head
                out_rest[:, place, pl.ds(at, 16), :] = rest


def tile_kernel(tiles_across, slabs, count, resident, over, tiles_ref, pos_ref, taps_ref, h_head, h_rest, e_head, e_rest, out_ref, rows_head, rows_rest):
    extent = tiles_across * TILE
    samples = pos_ref.shape[2]
    dot = functools.partial(jnp.dot, preferred_element_type=jnp.float32)
    slab = lax.axis_index("wa")
    cell = lax.broadcasted_iota(jnp.int32, (1, TILE), 1)
    angle = ((cell * slab) % slabs).astype(jnp.float32) * (-2.0 * math.pi / slabs)
    turn_real = jnp.cos(angle) * (1.0 / extent)
    turn_imag = jnp.sin(angle) * (1.0 / extent)
    place = lax.broadcasted_iota(jnp.int32, (TILE, 128), 0)
    u_start = place * over + over - 1
    groups = tiles_across
    per = TILE // groups
    v_start = ((place % per) * groups + place // per) * over + over - 1
    table = jnp.broadcast_to(taps_ref[...], (TILE, 128))

    def weights(start, position):
        index = start - position
        inside = (index & -128) == 0
        found = jnp.take_along_axis(table, index & 127, axis=1, mode="promise_in_bounds")
        return jnp.where(inside, found, 0.0)

    def one_block(block, row_tile, col_tile):
        head = h_head[col_tile]
        table_head = e_head[row_tile]
        both = dot(head, table_head) + dot(head, e_rest[row_tile]) + dot(h_rest[col_tile], table_head)
        real = both[:TILE, :TILE] - both[TILE:, TILE:]
        imag = both[:TILE, TILE:] + both[TILE:, :TILE]
        grid = jnp.concatenate(
            [real * turn_real - imag * turn_imag, real * turn_imag + imag * turn_real], axis=0
        )
        grid_head, grid_rest = halves(grid)
        for lane in range(0, samples, 128):
            head, rest = halves(weights(u_start, pos_ref[block, 0:1, pl.ds(lane, 128)]))
            rows_head[:, lane : lane + 128] = head
            rows_rest[:, lane : lane + 128] = rest
        head = rows_head[...]
        part = dot(grid_head, head) + dot(grid_head, rows_rest[...]) + dot(grid_rest, head)
        for lane in range(0, samples, 128):
            column = weights(v_start, pos_ref[block, 1:2, pl.ds(lane, 128)])
            for c in range(2):
                values = part[c * TILE : (c + 1) * TILE, lane : lane + 128] * column
                out_ref[block, c : c + 1, lane : lane + 128] = jnp.sum(values, axis=0, keepdims=True)

    if resident:

        @pl.loop(0, count)
        def _(block):
            tile = tiles_ref[block]
            one_block(block, tile // tiles_across, tile % tiles_across)

    else:
        one_block(0, 0, 0)


def shards(sky_model, plane_w, kernel, tile_ids, plane_ids, positions, observed):
    extent, columns = sky_model.shape[1:]
    planes, slabs = lax.axis_size("ba"), lax.axis_size("wa")
    devices = planes * slabs
    block_count, _, samples = positions.shape
    tiles_across = extent // TILE
    capacity = max(2, block_count // planes)
    slots = planes * capacity

    target = plane_ids[:, 0]
    same = target[:, None] == target[None, :]
    before = np.tril(np.ones((block_count, block_count), bool), -1)
    rank = jnp.sum((same & before).astype(jnp.int32), axis=1)
    slot_index = target * capacity + rank
    chosen = slot_index[:, None] == jnp.arange(slots, dtype=jnp.int32)[None, :]
    record = jnp.concatenate(
        [
            positions.reshape(block_count, 2 * samples),
            jnp.broadcast_to(tile_ids[:, None], (block_count, 128)),
        ],
        axis=1,
    )
    length = record.shape[1]
    asked = jnp.sum(jnp.where(chosen[:, :, None], record[:, None, :], 0), axis=0)
    asked = jnp.broadcast_to(
        asked.reshape(planes, 1, capacity, length), (planes, slabs, capacity, length)
    ).reshape(devices, capacity, length)
    axes = ("ba", "wa")
    asked = lax.all_to_all(asked, axes, split_axis=0, concat_axis=0, tiled=True)
    count = devices * capacity
    asked = asked.reshape(count, length)
    asked_fine = asked[:, : 2 * samples].reshape(count, 2, samples)
    asked_tiles = asked[:, 2 * samples]

    lanes = min(columns, 256)
    share = tiles_across * 8 // TILE
    folded = (tiles_across // share, share)
    y_head, y_rest = y_tables(extent)
    vmem = pl.BlockSpec(memory_space=pltpu.VMEM)
    h_head, h_rest = pl.pallas_call(
        functools.partial(y_kernel, extent, columns),
        grid=(columns // lanes,),
        in_specs=[
            pl.BlockSpec(memory_space=pltpu.SMEM),
            pl.BlockSpec((2, extent, lanes), lambda i: (0, 0, i)),
            pl.BlockSpec(y_head.shape, lambda i: (0, 0, 0), pipeline_mode=pl.Buffered(1)),
            pl.BlockSpec(y_rest.shape, lambda i: (0, 0, 0), pipeline_mode=pl.Buffered(1)),
        ],
        out_specs=[pl.BlockSpec(folded + (2 * TILE, lanes), lambda i: (0, 0, 0, i))] * 2,
        out_shape=[jax.ShapeDtypeStruct(folded + (2 * TILE, columns), jnp.bfloat16)] * 2,
        scratch_shapes=[pltpu.VMEM((tiles_across, 2 * TILE, lanes), jnp.float32)],
        compiler_params=pltpu.CompilerParams(vmem_limit_bytes=60 << 20),
        cost_estimate=pl.CostEstimate(
            flops=24 * extent * TILE * columns, bytes_accessed=32 * extent * columns, transcendentals=0
        ),
        name="y_transform",
    )(plane_w, sky_model, jnp.asarray(y_head), jnp.asarray(y_rest))
    h_head = h_head.reshape(tiles_across, 2 * TILE, columns)
    h_rest = h_rest.reshape(tiles_across, 2 * TILE, columns)

    over, support = kernel.shape
    taps = kernel[::-1, :].T.reshape(1, over * support)
    e_head, e_rest = x_tables(extent, columns)
    resident = 4 * tiles_across * 4 * TILE * columns * 2 <= 40 << 20
    if resident:
        layout = {
            "in_specs": [pl.BlockSpec(memory_space=pltpu.SMEM)] + [vmem] * 6,
            "out_specs": vmem,
            "scratch_shapes": [pltpu.VMEM((TILE, samples), jnp.bfloat16)] * 2,
        }
    else:
        own = pl.BlockSpec((1, 2, samples), lambda i, t: (i, 0, 0))
        side = pl.BlockSpec((1, 2 * TILE, columns), lambda i, t: (t[i] % tiles_across, 0, 0))
        table = pl.BlockSpec((1, columns, 2 * TILE), lambda i, t: (t[i] // tiles_across, 0, 0))
        layout = {
            "grid_spec": pltpu.PrefetchScalarGridSpec(
                num_scalar_prefetch=1,
                grid=(count,),
                in_specs=[own, vmem, side, side, table, table],
                out_specs=own,
                scratch_shapes=[pltpu.VMEM((TILE, samples), jnp.bfloat16)] * 2,
            )
        }
    values = pl.pallas_call(
        functools.partial(tile_kernel, tiles_across, slabs, count, resident, over),
        **layout,
        out_shape=jax.ShapeDtypeStruct((count, 2, samples), jnp.float32),
        compiler_params=pltpu.CompilerParams(vmem_limit_bytes=60 << 20),
        cost_estimate=pl.CostEstimate(
            flops=count * 12 * TILE * TILE * (columns + samples), bytes_accessed=32 << 20, transcendentals=0
        ),
        name="tile_degrid",
    )(asked_tiles, asked_fine, taps, h_head, h_rest, jnp.asarray(e_head), jnp.asarray(e_rest))

    values = values.reshape(devices, capacity, 2 * samples)
    answers = lax.all_to_all(values, axes, split_axis=0, concat_axis=0, tiled=True)
    answers = jnp.sum(answers.reshape(planes, slabs, capacity, 2 * samples), axis=1)
    answers = answers.reshape(slots, 2 * samples)
    predicted = jnp.sum(jnp.where(chosen[:, :, None], answers[None], 0.0), axis=1)
    return observed - predicted.reshape(observed.shape)


def solution(mesh):
    return jax.shard_map(
        shards,
        mesh=mesh,
        in_specs=(
            P(None, None, "wa"),
            P("ba"),
            P(),
            P(("ba", "wa")),
            P(("ba", "wa"), None),
            P(("ba", "wa"), None, None),
            P(("ba", "wa"), None, None),
        ),
        out_specs=P(("ba", "wa"), None, None),
        check_vma=False,
    )
```

time: 583 us -> 132 us (0.23); the launches traced: 576 us -> 132 us
  matrix products: 231 us -> 0 us
  waiting for transfers between devices: 185 us -> 0.01 us
  local copies, waits for them, and re-layouts: 112 us -> 6.96 us
  Pallas kernels: 0 us -> 98.4 us
  other arithmetic: 27.1 us -> 2.8 us
  blocking collectives: 0 us -> 15.9 us
  starting transfers between devices: 19 us -> 7.33 us
    dot_general x22 -> x0, matrix products: 231 us -> none  [product(): return jnp.einsum(pattern, operand_a, operand_b, precision=PRECISE)]
    all_to_all x4 -> x1, waiting for transfers between devices: 185 us -> 0.01 us  [shards(): asked = lax.all_to_all(asked, axes, split_axis=0, concat_axis=0, tiled=True)]
    pallas_call x0 -> x2, Pallas kernels: none -> 98.4 us  [the longest x1 75.8 us: shards(): pl.pallas_call(functools.partial(tile_kernel, tiles_across, slabs, count,...]
    gather x49 -> x0, local copies, waits for them, and re-layouts: 47.7 us -> none
    slice x8 -> x2, local copies, waits for them, and re-layouts: 23.2 us -> 0.64 us  [the longest x1 0.63 us: shards(): asked_tiles = asked[:, 2 * samples]]
    add x6 -> x1, other arithmetic: 18 us -> 0.66 us  [shards(): slot_index = target * capacity + rank]
    another operation x4 -> x0, local copies, waits for them, and re-layouts: 16.6 us -> none  [the longest x1 16.5 us: shards(): jnp.stack([half_done[0].reshape(column_count, extent), half_done[1].resha...]
    all_to_all x0 -> x1, blocking collectives: none -> 15.9 us  [shards(): lax.all_to_all(values, axes, split_axis=0, concat_axis=0, tiled=True)]
  transfers between devices with their start and end apart: 4 -> 1, of which waited for: 2 -> 0; matrix products, arithmetic and copies ran while one was open for 45% -> 1% of each run, Pallas kernels for 0% -> 17%
where the time goes in v1:
time: 132 us
  Pallas kernels  98.4 us (75%)
  blocking collectives  15.9 us (12%)
  starting transfers between devices  7.33 us (6%)
  local copies, waits for them, and re-layouts  6.96 us (5%)
  other arithmetic  2.8 us (2%)
    pallas_call x1, Pallas kernels, shards(): pl.pallas_call(functools.partial(tile_kernel, tiles_across, slabs, count,...  75.8 us
    pallas_call x1, Pallas kernels, shards(): pl.pallas_call(functools.partial(y_kernel, extent, columns), grid=(column...  22.6 us
    all_to_all x1, blocking collectives, shards(): lax.all_to_all(values, axes, split_axis=0, concat_axis=0, tiled=True)  15.9 us
    all_to_all x1, starting transfers between devices, shards(): asked = lax.all_to_all(asked, axes, split_axis=0, concat_axis=0, tiled=True)  7.33 us
  transfers between devices with their start and end apart: 1, of which 0 were waited for; matrix products, arithmetic and copies ran while one was open for 1% of the time, Pallas kernels for 17%

profile of v1, /device:TPU:0, one launch (start us, length us, event | category | flops | bytes accessed | tf_op | source)
XLA Modules:
  0.0 132.1 jit_solution(2361543411110180333)
XLA Ops:
  0.0 0.9 convert_reduce_fusion
  0.9 0.7 fusion
  1.6 0.1 iota_compare_fusion
  1.7 0.9 copy.14
  2.5 0.7 broadcast_in_dim.62
  3.2 0.1 select_reduce_fusion
  3.4 0.8 broadcast_in_dim.66
  4.3 7.3 %all-to-all-start = ((s32[32,2,1152]{2,1,0:T(2,128)}), s32[32,2,1152]{2,1,0:T(2,128)S(1)}, u32[]{:S(2)}, u32[]{:S(2)}) async-start(s32[32,2,1152]{2,1,0:T(2,128)} %bitcast.3), calls=%async_computation | async-start | bytes 589824 | tf_op jit(solution)/shard_map/all_to_all | solution.py:238
  12.2 0.8 rev.3
  13.0 0.6 reshape.63.taps_ref
  13.6 22.6 %y_transform.1 = (bf16[16,1,256,512]{3,2,1,0:T(8,128)(2,1)}, bf16[16,1,256,512]{3,2,1,0:T(8,128)(2,1)}) custom-call(f32[1]{0:T(128)S(6)} %copy.15.w_ref, f32[2,2048,512]{2,1,0:T(8,128)} %sky_ref.1, bf16[16,256,256]{2,1,0:T(8,128)(2,1)} %constant.17.clone.head_ref, bf16[16,256,256]{2,1,0:T(8,128)(2,1)} %constant.18.clone.rest_ref), custom_call_target="tpu_custom_call" | custom-call | flops 3221225472 | bytes 33554432 | tf_op jit(solution)/shard_map/y_transform/pallas_call | solution.py:249
  36.2 0.0 all-to-all-done
  36.2 0.2 reshape.61
  36.4 0.6 slice_reduce_fusion.tiles_ref
  37.1 0.9 reshape.62.pos_ref
  38.0 0.0 copy-start
  38.0 75.8 %tile_degrid.1 = f32[64,2,512]{2,1,0:T(2,128)} custom-call(s32[64]{0:T(128)} %slice_reduce_fusion.tiles_ref, s32[64,2,512]{2,1,0:T(2,128)} %reshape.62.pos_ref, f32[1,128]{1,0:T(1,128)} %reshape.63.taps_ref, bf16[16,256,512]{2,1,0:T(8,128)(2,1)} %bitcast.19, bf16[16,256,512]{2,1,0:T(8,128)(2,1)} %bitcast.20, bf16[16,512,256]{2,1,0:T(8,128)(2,1)} %constant.19.clone.e_head, ...), custom_call_target="tpu_custom_call" | custom-call | flops 12884901888 | bytes 33554432 | tf_op jit(solution)/shard_map/tile_degrid/pallas_call | solution.py:293
  113.8 1.3 reshape.66
  115.1 15.9 %all_to_all.10 = f32[32,2,1024]{2,1,0:T(2,128)S(1)} all-to-all(f32[32,2,1024]{2,1,0:T(2,128)S(1)} %reshape.66), channel_id=1, replica_groups=mesh['ba'=8,'wa'=4] {'ba','wa'}, dimensions={0} | all-to-all | bytes 524288 | tf_op jit(solution)/shard_map/all_to_all | solution.py:305
  131.0 0.1 bitcast_reduce_fusion
  131.1 0.3 select_reduce_fusion.1
  131.4 0.1 reshape.68
  131.4 0.0 copy-done
  131.4 0.7 sub.3
  (4 shorter events, 0.1 us)
Async XLA Ops:
  4.3 32.0 %all-to-all-start = ((s32[32,2,1152]{2,1,0:T(2,128)}), s32[32,2,1152]{2,1,0:T(2,128)S(1)}, u32[]{:S(2)}, u32[]{:S(2)}) async-start(s32[32,2,1152]{2,1,0:T(2,128)} %bitcast.3), calls=%async_computation | async-start | bytes 589824 | tf_op jit(solution)/shard_map/all_to_all | solution.py:238
  38.0 93.4 %copy-start = (f32[16,2,512]{2,1,0:T(2,128)S(1)}, f32[16,2,512]{2,1,0:T(2,128)}, u32[]{:S(2)}) copy-start(f32[16,2,512]{2,1,0:T(2,128)} %param.18) | copy-start | bytes 196612

commit v2 on v1

v2 whole, which is shorter than its diff:
```python
import functools
import math

import jax
import jax.numpy as jnp
import numpy as np
from jax import lax
from jax.experimental import pallas as pl
from jax.experimental.pallas import tpu as pltpu
from jax.sharding import PartitionSpec as P

TILE = 128
FIELD_WIDTH = 0.7


def halves(values):
    head = values.astype(jnp.bfloat16)
    rest = (values - head.astype(jnp.float32)).astype(jnp.bfloat16)
    return head, rest


def host_halves(values):
    values = values.astype(np.float32)
    head = values.astype(jnp.bfloat16)
    rest = (values - head.astype(np.float32)).astype(jnp.bfloat16)
    return head, rest


def roots(index, modulus):
    angle = -2.0 * np.pi * (index % modulus) / modulus
    return np.cos(angle), np.sin(angle)


def y_tables(extent):
    panels = extent // TILE
    residue = np.arange(panels, dtype=np.int64)[:, None, None]
    step = np.arange(TILE, dtype=np.int64)[None, :, None]
    row = np.arange(TILE, dtype=np.int64)[None, None, :]
    real, imag = roots((panels * step + residue) * row, extent)
    table = np.concatenate(
        [np.concatenate([real, -imag], axis=2), np.concatenate([imag, real], axis=2)], axis=1
    )
    return host_halves(table)


def x_tables(extent, columns):
    tiles = np.arange(extent // TILE, dtype=np.int64)[:, None, None]
    column = np.arange(columns, dtype=np.int64)[None, :, None]
    cell = np.arange(TILE, dtype=np.int64)[None, None, :]
    real, imag = roots((tiles * TILE + cell) * column, extent)
    return host_halves(np.concatenate([real, imag], axis=2))


def fit(function, top, terms):
    nodes = (np.cos((np.arange(400) + 0.5) * np.pi / 400) + 1.0) * 0.5 * top
    series = np.polynomial.chebyshev.Chebyshev.fit(nodes, function(nodes), terms - 1, domain=[0, top])
    return [float(c) for c in series.convert(kind=np.polynomial.Polynomial).coef]


def horner(coefficients, argument):
    total = coefficients[-1]
    for coefficient in coefficients[-2::-1]:
        total = total * argument + coefficient
    return total


def small_dft(values):
    count = len(values)
    if count == 1:
        return values
    even = small_dft(values[0::2])
    odd = small_dft(values[1::2])
    low, high = [], []
    for k in range(count // 2):
        real, imag = odd[k]
        if k == 0:
            pass
        elif 4 * k == count:
            real, imag = imag, -real
        elif 8 * k == count:
            h = math.sqrt(0.5)
            real, imag = (real + imag) * h, (imag - real) * h
        elif 8 * k == 3 * count:
            h = math.sqrt(0.5)
            real, imag = (imag - real) * h, (real + imag) * -h
        else:
            c = math.cos(-2.0 * math.pi * k / count)
            s = math.sin(-2.0 * math.pi * k / count)
            real, imag = real * c - imag * s, real * s + imag * c
        low.append((even[k][0] + real, even[k][1] + imag))
        high.append((even[k][0] - real, even[k][1] - imag))
    return low + high


def lane_lookup(table, index):
    numbers = lax.GatherDimensionNumbers(
        offset_dims=(),
        collapsed_slice_dims=(1,),
        start_index_map=(1,),
        operand_batching_dims=(0,),
        start_indices_batching_dims=(0,),
    )
    return lax.gather(
        table, index[..., None], numbers, (1, 1), mode=lax.GatherScatterMode.PROMISE_IN_BOUNDS
    )


def dot_exact(head_a, rest_a, head_b, rest_b):
    return jnp.dot(
        jnp.concatenate([head_a, head_a, rest_a], axis=1),
        jnp.concatenate([head_b, rest_b, head_b], axis=0),
        preferred_element_type=jnp.float32,
    )


def y_transform(extent, first, w, sky_ref, work):
    panels = extent // TILE
    lanes = sky_ref.shape[2]
    spacing = FIELD_WIDTH / extent
    edge = 2.0 * (FIELD_WIDTH / 2) ** 2
    lower = fit(lambda r: 1.0 / (1.0 + np.sqrt(1.0 - r)), edge, 7)
    sine = fit(lambda z: np.sin(2 * np.pi * np.sqrt(z)) / np.sqrt(z), 0.25, 7)
    cosine = fit(lambda z: np.cos(2 * np.pi * np.sqrt(z)), 0.25, 7)

    for lane in range(0, lanes, 128):
        x = lax.broadcasted_iota(jnp.int32, (8, 128), 1) + (first + lane)
        x = (x.astype(jnp.float32) - extent / 2) * spacing
        x_sq = x * x

        @pl.loop(0, TILE // 8)
        def _(group):
            base = pl.multiple_of(group * 8, 8)
            values = []
            for panel in range(panels):
                row = lax.broadcasted_iota(jnp.int32, (8, 128), 0) + (base + panel * TILE)
                y = (row.astype(jnp.float32) - extent / 2) * spacing
                radius = x_sq + y * y
                turns = radius * horner(lower, radius) * w
                turns = turns - jnp.round(turns)
                square = turns * turns
                s = turns * horner(sine, square)
                c = horner(cosine, square)
                real = sky_ref[0, pl.ds(base + panel * TILE, 8), pl.ds(lane, 128)]
                imag = sky_ref[1, pl.ds(base + panel * TILE, 8), pl.ds(lane, 128)]
                values.append((real * c - imag * s, real * s + imag * c))
            for residue, (real, imag) in enumerate(small_dft(values)):
                work[residue, pl.ds(base, 8), pl.ds(lane, 128)] = real
                work[residue, pl.ds(base + TILE, 8), pl.ds(lane, 128)] = imag


def y_finish(extent, start, work, table_head, table_rest, h_head, h_rest):
    panels = extent // TILE
    lanes = work.shape[2]
    per_tile = TILE // panels
    share = 8 // per_tile
    together = 16 // per_tile

    @pl.loop(0, panels // together)
    def _(step):
        products = []
        for i in range(together):
            residue = together * step + i
            head, rest = halves(work[residue])
            products.append(dot_exact(table_head[residue], table_rest[residue], head, rest))
        for part in range(2):
            rows = slice(part * TILE, (part + 1) * TILE)
            grouped = [product[rows].reshape(TILE // 8, 8, lanes) for product in products]
            at = pl.multiple_of(part * TILE + step * 16, 16)
            for place in range(share):
                cut = slice(place * per_tile, (place + 1) * per_tile)
                head, rest = halves(jnp.concatenate([group[:, cut] for group in grouped], axis=1))
                h_head[:, place, pl.ds(at, 16), pl.ds(start, lanes)] = head
                h_rest[:, place, pl.ds(at, 16), pl.ds(start, lanes)] = rest


def plane_kernel(
    extent, slabs, over, unroll,
    tiles_ref, w_ref, sky_ref, asked_ref, taps_ref, y_head, y_rest, e_head, e_rest, out_ref,
    work, h_head, h_rest, yh, yr, eh, er, rows_head, rows_rest, sems,
):
    tiles_across = extent // TILE
    columns = eh.shape[1]
    lanes = sky_ref.shape[2]
    chunk = pl.program_id(0)
    slab = lax.axis_index("wa")
    share = h_head.shape[1]
    copies = [
        pltpu.make_async_copy(source, target, sems.at[i])
        for i, (source, target) in enumerate(((y_head, yh), (y_rest, yr), (e_head, eh), (e_rest, er)))
    ]

    @pl.when(chunk == 0)
    def _():
        for copy in copies:
            copy.start()

    y_transform(extent, slab * columns + chunk * lanes, w_ref[0], sky_ref, work)

    @pl.when(chunk == 0)
    def _():
        copies[0].wait()
        copies[1].wait()

    y_finish(extent, pl.multiple_of(chunk * lanes, lanes), work, yh, yr, h_head, h_rest)

    @pl.when(chunk == columns // lanes - 1)
    def _():
        copies[2].wait()
        copies[3].wait()
        owners, capacity, length = out_ref.shape
        samples = length // 2
        cell = lax.broadcasted_iota(jnp.int32, (1, TILE), 1)
        angle = ((cell * slab) % slabs).astype(jnp.float32) * (-2.0 * math.pi / slabs)
        turn_real = jnp.cos(angle) * (1.0 / extent)
        turn_imag = jnp.sin(angle) * (1.0 / extent)
        per = TILE // tiles_across

        def weights(axis, position):
            place = lax.broadcasted_iota(jnp.int32, (TILE, 128), 0)
            if axis == 1:
                place = (place % per) * tiles_across + place // per
            index = place * over + (over - 1) - position
            table = jnp.broadcast_to(taps_ref[...], (TILE, 128))
            return jnp.where((index & -128) == 0, lane_lookup(table, index & 127), 0.0)

        def form_tile(tile):
            row_tile = tile // tiles_across
            col_tile = tile % tiles_across
            group, place = col_tile // share, col_tile % share
            both = dot_exact(h_head[group, place], h_rest[group, place], eh[row_tile], er[row_tile])
            real = both[:TILE, :TILE] - both[TILE:, TILE:]
            imag = both[:TILE, TILE:] + both[TILE:, :TILE]
            return halves(
                jnp.concatenate(
                    [real * turn_real - imag * turn_imag, real * turn_imag + imag * turn_real], axis=0
                )
            )

        def row_weights(spot, owner, place):
            for lane in range(0, samples, 128):
                head, rest = halves(weights(0, asked_ref[owner, place : place + 1, lane : lane + 128]))
                rows_head[spot, :, lane : lane + 128] = head
                rows_rest[spot, :, lane : lane + 128] = rest

        def predict(spot, owner, place, tile_pair):
            part = dot_exact(*tile_pair, rows_head[spot], rows_rest[spot])
            for lane in range(0, samples, 128):
                at = samples + lane
                column = weights(1, asked_ref[owner, place : place + 1, at : at + 128])
                for c in range(2):
                    values = part[c * TILE : (c + 1) * TILE, lane : lane + 128] * column
                    at = c * samples + lane
                    out_ref[owner, place : place + 1, at : at + 128] = jnp.sum(
                        values, axis=0, keepdims=True
                    )

        @pl.loop(0, owners // unroll)
        def _(step):
            work_list = [(step * unroll + o, c) for o in range(unroll) for c in range(capacity)]
            tiles = [tiles_ref[owner * capacity + c] for owner, c in work_list]
            pairs = {}
            for spot, (owner, c) in enumerate(work_list):
                row_weights(spot, owner, c)
                pairs[spot] = form_tile(tiles[spot])
                if spot:
                    predict(spot - 1, *work_list[spot - 1], pairs.pop(spot - 1))
            predict(spot, *work_list[spot], pairs.pop(spot))


def pack_kernel(planes_ref, tiles_ref, pos_ref, out_ref, used):
    planes, slabs, capacity, length = out_ref.shape
    blocks, _, samples = pos_ref.shape
    for p in range(planes):
        used[p] = 0

    @pl.loop(0, planes)
    def _(p):
        for a in range(slabs):
            out_ref[p, a] = jnp.zeros((capacity, length), jnp.int32)

    @pl.loop(0, blocks)
    def _(b):
        p = planes_ref[b]
        k = used[p]
        used[p] = k + 1
        for place in range(capacity):

            @pl.when(k == place)
            def _():
                for a in range(slabs):
                    for axis in range(2):
                        cut = slice(axis * samples, (axis + 1) * samples)
                        out_ref[p, a, place : place + 1, cut] = pos_ref[b, axis : axis + 1, :]
                    out_ref[p, a, place : place + 1, 2 * samples :] = jnp.full(
                        (1, 128), tiles_ref[b], jnp.int32
                    )


def residual_kernel(planes, slabs, planes_ref, answers_ref, observed_ref, out_ref, used):
    blocks, _, samples = observed_ref.shape
    for p in range(planes):
        used[p] = 0

    @pl.loop(0, blocks)
    def _(b):
        p = planes_ref[b]
        k = used[p]
        used[p] = k + 1
        total = answers_ref[p * slabs]
        for a in range(1, slabs):
            total += answers_ref[p * slabs + a]
        own = total[0:1]
        for place in range(1, total.shape[0]):
            own = jnp.where(k == place, total[place : place + 1], own)
        for c in range(2):
            out_ref[b, c : c + 1, :] = (
                observed_ref[b, c : c + 1, :] - own[:, c * samples : (c + 1) * samples]
            )


def shards(sky_model, plane_w, kernel, tile_ids, plane_ids, positions, observed):
    extent, columns = sky_model.shape[1:]
    planes, slabs = lax.axis_size("ba"), lax.axis_size("wa")
    devices = planes * slabs
    block_count, _, samples = positions.shape
    tiles_across = extent // TILE
    capacity = max(2, block_count // planes)
    target = plane_ids[:, 0]
    axes = ("ba", "wa")
    smem = pl.BlockSpec(memory_space=pltpu.SMEM)
    vmem = pl.BlockSpec(memory_space=pltpu.VMEM)
    hbm = pl.BlockSpec(memory_space=pl.ANY)
    length = 2 * samples + 128

    asked = pl.pallas_call(
        pack_kernel,
        in_specs=[smem, smem, vmem],
        out_specs=vmem,
        out_shape=jax.ShapeDtypeStruct((planes, slabs, capacity, length), jnp.int32),
        scratch_shapes=[pltpu.SMEM((planes,), jnp.int32)],
        name="pack",
    )(target, tile_ids, positions)
    asked = asked.reshape(devices, capacity, length)
    asked = lax.all_to_all(asked, axes, split_axis=0, concat_axis=0, tiled=True)
    asked_tiles = asked[:, :, 2 * samples].reshape(devices * capacity)

    lanes = min(columns, 256)
    share = tiles_across * 8 // TILE
    unroll = 2
    over, support = kernel.shape
    taps = kernel[::-1, :].T.reshape(1, over * support)
    y_head, y_rest = y_tables(extent)
    e_head, e_rest = x_tables(extent, columns)
    once = pl.Buffered(1)
    answer_shape = (devices, capacity, 2 * samples)
    half = jnp.bfloat16
    values = pl.pallas_call(
        functools.partial(plane_kernel, extent, slabs, over, unroll),
        grid=(columns // lanes,),
        in_specs=[
            smem,
            smem,
            pl.BlockSpec((2, extent, lanes), lambda i: (0, 0, i)),
            pl.BlockSpec(asked.shape, lambda i: (0, 0, 0), pipeline_mode=once),
            pl.BlockSpec(taps.shape, lambda i: (0, 0), pipeline_mode=once),
            hbm, hbm, hbm, hbm,
        ],
        out_specs=pl.BlockSpec(answer_shape, lambda i: (0, 0, 0)),
        out_shape=jax.ShapeDtypeStruct(answer_shape, jnp.float32),
        scratch_shapes=[
            pltpu.VMEM((tiles_across, 2 * TILE, lanes), jnp.float32),
            pltpu.VMEM((tiles_across // share, share, 2 * TILE, columns), half),
            pltpu.VMEM((tiles_across // share, share, 2 * TILE, columns), half),
            pltpu.VMEM(y_head.shape, half),
            pltpu.VMEM(y_head.shape, half),
            pltpu.VMEM(e_head.shape, half),
            pltpu.VMEM(e_head.shape, half),
            pltpu.VMEM((unroll * capacity, TILE, samples), half),
            pltpu.VMEM((unroll * capacity, TILE, samples), half),
            pltpu.SemaphoreType.DMA((4,)),
        ],
        compiler_params=pltpu.CompilerParams(vmem_limit_bytes=60 << 20),
        name="plane",
    )(
        asked_tiles, plane_w, sky_model, asked, taps,
        jnp.asarray(y_head), jnp.asarray(y_rest), jnp.asarray(e_head), jnp.asarray(e_rest),
    )

    answers = lax.all_to_all(values, axes, split_axis=0, concat_axis=0, tiled=True)
    return pl.pallas_call(
        functools.partial(residual_kernel, planes, slabs),
        in_specs=[smem, vmem, vmem],
        out_specs=vmem,
        out_shape=jax.ShapeDtypeStruct(observed.shape, jnp.float32),
        scratch_shapes=[pltpu.SMEM((planes,), jnp.int32)],
        name="residual",
    )(target, answers, observed)


def solution(mesh):
    return jax.shard_map(
        shards,
        mesh=mesh,
        in_specs=(
            P(None, None, "wa"),
            P("ba"),
            P(),
            P(("ba", "wa")),
            P(("ba", "wa"), None),
            P(("ba", "wa"), None, None),
            P(("ba", "wa"), None, None),
        ),
        out_specs=P(("ba", "wa"), None, None),
        check_vma=False,
    )
```

time: 132 us -> 85.7 us (0.65)
  Pallas kernels: 98.4 us -> 52.6 us
  waiting for transfers between devices: 0.01 us -> 8.66 us
  local copies, waits for them, and re-layouts: 6.96 us -> 2.62 us
  other arithmetic: 2.8 us -> 0 us
  blocking collectives: 15.9 us -> 13.5 us
    pallas_call x2 -> x3, Pallas kernels: 98.4 us -> 52.6 us  [the longest x1 48.7 us: shards(): pl.pallas_call(functools.partial(plane_kernel, extent, slabs, over, unrol...]
    all_to_all x1, waiting for transfers between devices: 0.01 us -> 8.66 us  [shards(): asked = lax.all_to_all(asked, axes, split_axis=0, concat_axis=0, tiled=True)]
    reshape x4 -> x0, local copies, waits for them, and re-layouts: 2.45 us -> none  [the longest x1 1.26 us: shards(): values = values.reshape(devices, capacity, 2 * samples)]
    all_to_all x1, blocking collectives: 15.9 us -> 13.5 us  [shards(): lax.all_to_all(values, axes, split_axis=0, concat_axis=0, tiled=True)]
    broadcast_in_dim x4 -> x0, local copies, waits for them, and re-layouts: 1.63 us -> none  [the longest x2 0.86 us: shards(): jnp.broadcast_to(asked.reshape(planes, 1, capacity, length), (planes, sla...]
    reduce_sum x4 -> x0, other arithmetic: 1.39 us -> none  [the longest x1 0.91 us: shards(): rank = jnp.sum((same & before).astype(jnp.int32), axis=1)]
  transfers between devices with their start and end apart: 1 -> 1, of which waited for: 0 -> 1; matrix products, arithmetic and copies ran while one was open for 1% -> 2% of each run, Pallas kernels for 17% -> 0%
where the time goes in v2:
time: 85.7 us; the launch traced here: 85.4 us
  Pallas kernels  52.6 us (61%)
  blocking collectives  13.5 us (16%)
  waiting for transfers between devices  8.66 us (10%)
  starting transfers between devices  7.33 us (9%)
  local copies, waits for them, and re-layouts  2.62 us (3%)
    pallas_call x1, Pallas kernels, shards(): pl.pallas_call(functools.partial(plane_kernel, extent, slabs, over, unrol...  48.7 us
    all_to_all x1, blocking collectives, shards(): lax.all_to_all(values, axes, split_axis=0, concat_axis=0, tiled=True)  13.5 us
    all_to_all x1, waiting for transfers between devices, shards(): asked = lax.all_to_all(asked, axes, split_axis=0, concat_axis=0, tiled=True)  8.66 us
    all_to_all x1, starting transfers between devices, shards(): asked = lax.all_to_all(asked, axes, split_axis=0, concat_axis=0, tiled=True)  7.33 us
    pallas_call x1, Pallas kernels, shards(): pl.pallas_call(pack_kernel, in_specs=[smem, smem, vmem], out_specs=vmem,...  2.01 us
    pallas_call x1, Pallas kernels, shards(): pl.pallas_call(functools.partial(residual_kernel, planes, slabs), in_spec...  1.82 us
  transfers between devices with their start and end apart: 1, of which 1 were waited for; matrix products, arithmetic and copies ran while one was open for 2% of the time, Pallas kernels for 0%

profile of v2, /device:TPU:0, one launch (start us, length us, event | category | flops | bytes accessed | tf_op | source)
XLA Modules:
  0.0 85.4 jit_solution(5926836150339558523)
XLA Ops:
  0.0 2.0 %pack.1 = s32[8,4,2,1152]{3,2,1,0:T(2,128)} custom-call(s32[16]{0:T(128)} %bitcast.5, s32[16]{0:T(128)} %tiles_ref.1, s32[16,2,512]{2,1,0:T(2,128)} %pos_ref.1), custom_call_target="tpu_custom_call" | custom-call | tf_op jit(solution)/shard_map/pack/pallas_call | solution.py:335
  2.0 7.3 %all-to-all-start = ((s32[32,2,1152]{2,1,0:T(2,128)}), s32[32,2,1152]{2,1,0:T(2,128)S(1)}, u32[]{:S(2)}, u32[]{:S(2)}) async-start(s32[32,2,1152]{2,1,0:T(2,128)} %bitcast.3), calls=%async_computation | async-start | bytes 589824 | tf_op jit(solution)/shard_map/all_to_all | solution.py:344
  9.3 0.8 rev.3
  10.1 0.6 reshape.7.taps_ref
  11.4 8.7 %all-to-all-done.asked_ref = s32[32,2,1152]{2,1,0:T(2,128)S(1)} async-done(((s32[32,2,1152]{2,1,0:T(2,128)}), s32[32,2,1152]{2,1,0:T(2,128)S(1)}, u32[]{:S(2)}, u32[]{:S(2)}) %all-to-all-start) | async-done | bytes 294944 | tf_op jit(solution)/shard_map/all_to_all | solution.py:344
  20.0 0.0 copy-start
  20.0 0.6 slice_reduce_fusion
  20.7 0.6 reshape_squeeze.3.tiles_ref
  21.3 0.0 copy-done
  21.3 48.7 %plane.1 = f32[32,2,1024]{2,1,0:T(2,128)} custom-call(s32[64]{0:T(128)} %reshape_squeeze.3.tiles_ref, f32[1]{0:T(128)S(6)} %copy.12.w_ref, f32[2,2048,512]{2,1,0:T(8,128)} %sky_ref.1, s32[32,2,1152]{2,1,0:T(2,128)} %copy-done, f32[1,128]{1,0:T(1,128)} %reshape.7.taps_ref, bf16[16,256,256]{2,1,0:T(8,128)(2,1)} %constant.8.clone.y_head, ...), custom_call_target="tpu_custom_call" | custom-call | tf_op jit(solution)/shard_map/plane/pallas_call | solution.py:357
  70.0 13.5 %all_to_all.10.answers_ref = f32[32,2,1024]{2,1,0:T(2,128)} all-to-all(f32[32,2,1024]{2,1,0:T(2,128)} %plane.1), channel_id=1, replica_groups=mesh['ba'=8,'wa'=4] {'ba','wa'}, dimensions={0} | all-to-all | bytes 524288 | tf_op jit(solution)/shard_map/all_to_all | solution.py:389
  83.5 1.8 %residual.1 = f32[16,2,512]{2,1,0:T(2,128)} custom-call(s32[16]{0:T(128)} %bitcast.6, f32[32,2,1024]{2,1,0:T(2,128)} %all_to_all.10.answers_ref, f32[16,2,512]{2,1,0:T(2,128)} %observed_ref.1), custom_call_target="tpu_custom_call" | custom-call | tf_op jit(solution)/shard_map/residual/pallas_call | solution.py:390
Async XLA Ops:
  2.0 18.0 %all-to-all-start = ((s32[32,2,1152]{2,1,0:T(2,128)}), s32[32,2,1152]{2,1,0:T(2,128)S(1)}, u32[]{:S(2)}, u32[]{:S(2)}) async-start(s32[32,2,1152]{2,1,0:T(2,128)} %bitcast.3), calls=%async_computation | async-start | bytes 589824 | tf_op jit(solution)/shard_map/all_to_all | solution.py:344
  20.0 1.2 %copy-start = (s32[32,2,1152]{2,1,0:T(2,128)}, s32[32,2,1152]{2,1,0:T(2,128)S(1)}, u32[]{:S(2)}) copy-start(s32[32,2,1152]{2,1,0:T(2,128)S(1)} %all-to-all-done.asked_ref) | copy-start | bytes 884740
